TPU v7x, 256 devices: a whole 4x4x8 slice. The times are simulated.
256 devices in a mesh: grp: 4 (over z_lo), tp: 32 (over x, y, z_hi), rep: 2 (over core).
Axes of the slice: x: 4, y: 4, z: 8 (z_hi: 2, z_lo: 4; z = z_hi * 4 + z_lo), core: 2. Of those that a mesh axis runs over, the one named last changes fastest.
Arguments:
- query_rows: bfloat16 [32, 1024, 2048], P('tp', ('grp', 'rep')), may hold values from -120 to 120
- key_rows: bfloat16 [32, 1024, 512], P('tp', ('grp', 'rep')), may hold values from -6 to 6, as said below
- value_rows: bfloat16 [32, 1024, 512], P('tp', ('grp', 'rep')), may hold values from -6 to 6
- teacher_codes: bfloat16 [32, 1024, 4096], P(None, ('grp', 'rep'), 'tp'), may hold values from -6 to 6
- teacher_scales: bfloat16 [32, 1024, 32], P(None, ('grp', 'rep'), 'tp'), may hold values from 0.099609375 to 1
- projection: bfloat16 [2048, 4096], P(None, ('grp', 'rep')), may hold values from -0.125 to 0.125
Outputs:
- grad_query: bfloat16 [32, 1024, 2048], P('tp', ('grp', 'rep'))
- grad_key: bfloat16 [32, 1024, 512], P('tp', ('grp', 'rep'))
- grad_value: bfloat16 [32, 1024, 512], P('tp', ('grp', 'rep'))
Inputs may be any that keep to these rules, and one draw needn't show every extreme that they name: `key_rows`: keys of every head.
All inputs are finite; a program needn't handle non-finite values.
Results may differ from a plain program's by a relative error of at most 0.014.
Values may be sent and summed in bfloat16 or wider, within the bound.
No kernel may reach another device: no remote copies, remote signals or barrier semaphores. Data moves between devices by JAX's collectives and lax.ppermute only.
A program may use at most 128 MiB of HBM per device.

v0:
```python
import math
import jax
import jax.numpy as jnp
from jax import lax
from jax.sharding import PartitionSpec as P

HEADS = 16
KV_HEADS = 4
HEAD_DIM = 128
QBLOCK = 128
masked_low = -1e30


def in_one_piece(arrays, axis, dim, along):
    widths = [a.shape[along] for a in arrays]
    both = jnp.concatenate(arrays, axis=along)
    whole = lax.all_gather(both, axis, axis=dim, tiled=True)
    return tuple(jnp.split(whole, [sum(widths[:k]) for k in range(1, len(widths))], axis=along))


def in_one_piece_2(arrays, axis, dim, along):
    widths = [a.shape[along] for a in arrays]
    both = jnp.concatenate(arrays, axis=along)
    whole = lax.psum_scatter(both, axis, scatter_dimension=dim, tiled=True)
    return tuple(jnp.split(whole, [sum(widths[:k]) for k in range(1, len(widths))], axis=along))


def shards(query_rows, key_rows, value_rows, teacher_codes, teacher_scales, projection):
    rows_dev = query_rows.shape[1]
    group_size = HEADS // KV_HEADS
    inv_root = 1.0 / math.sqrt(HEAD_DIM)
    keys_all, values_all = in_one_piece((key_rows, value_rows), ("grp", "rep"), 1, 0)
    length = keys_all.shape[1]
    key_block = min(1024, length)
    my_index = lax.axis_index(("grp", "rep"))
    first_row = my_index * rows_dev
    needed = (first_row + rows_dev + key_block - 1) // key_block
    queries = query_rows[0].reshape(rows_dev, KV_HEADS, group_size, HEAD_DIM).transpose(1, 2, 0, 3)
    key_heads = keys_all[0].reshape(length, KV_HEADS, HEAD_DIM).transpose(1, 0, 2)
    value_heads = values_all[0].reshape(length, KV_HEADS, HEAD_DIM).transpose(1, 0, 2)
    row_pos = first_row + jnp.arange(rows_dev, dtype=jnp.int32)
    slab_codes, slab_scales = (
        lax.all_to_all(teacher_codes, "tp", split_axis=0, concat_axis=2, tiled=True),
        lax.all_to_all(teacher_scales, "tp", split_axis=0, concat_axis=2, tiled=True),
    )

    def block_scores(block_index):
        offset = block_index * key_block
        raw_scores = (
            jnp.einsum("hgqd,hkd->hgqk", queries, key_heads, preferred_element_type=jnp.float32)
            * inv_root
        )
        col_pos = offset + jnp.arange(key_block, dtype=jnp.int32)
        allowed = col_pos[None, :] <= row_pos[:, None]
        return (jnp.where(allowed, raw_scores, masked_low), key_heads, value_heads)

    def stats_step(block_index, running):
        row_peak, row_total = running
        scores, key_part, value_part = block_scores(block_index)
        new_peak = jnp.maximum(row_peak, scores.max(-1))
        row_total = row_total * jnp.exp(row_peak - new_peak) + jnp.exp(
            scores - new_peak[..., None]
        ).sum(-1)
        return (new_peak, row_total)

    stat_shape = (KV_HEADS, group_size, rows_dev)
    row_peak, row_total = lax.fori_loop(
        0,
        needed,
        stats_step,
        (jnp.full(stat_shape, masked_low, jnp.float32), jnp.zeros(stat_shape, jnp.float32)),
    )

    def block_probs(scores):
        return jnp.exp(scores - row_peak[..., None]) / row_total[..., None]

    def output_step(block_index, running):
        scores, key_part, value_part = block_scores(block_index)
        prob_low = block_probs(scores).astype(jnp.bfloat16)
        return running + jnp.einsum(
            "hgqk,hkd->hgqd", prob_low, value_part, preferred_element_type=jnp.float32
        )

    attn_wide = lax.fori_loop(
        0, needed, output_step, jnp.zeros((KV_HEADS, group_size, rows_dev, HEAD_DIM), jnp.float32)
    )
    attn_low = (
        attn_wide.transpose(2, 0, 1, 3).reshape(rows_dev, HEADS * HEAD_DIM).astype(jnp.bfloat16)
    )
    col_width = projection.shape[1]
    shard_piece = lax.all_gather(projection, ("grp", "rep"), axis=1, tiled=True)
    pieces = shard_piece.shape[1] // col_width
    shaped = shard_piece.reshape(shard_piece.shape[0], pieces, col_width)
    approx = jnp.einsum("td,dsc->tsc", attn_low, shaped, preferred_element_type=jnp.float32)
    code_rows = slab_codes[0].astype(jnp.float32)
    scale_rows = slab_scales[0].astype(jnp.float32)
    target = (code_rows.reshape(rows_dev, -1, QBLOCK) * scale_rows[..., None]).reshape(
        rows_dev, pieces, col_width
    )
    errors = (approx - target).astype(jnp.bfloat16)
    partial_terms = jnp.einsum(
        "tsc,dsc->std", errors, shaped, preferred_element_type=jnp.float32
    ).astype(jnp.bfloat16)
    grad_attn = partial_terms.astype(jnp.float32).sum(0)
    grad_low = grad_attn.astype(jnp.bfloat16)
    grad_heads = grad_low.reshape(rows_dev, KV_HEADS, group_size, HEAD_DIM).transpose(1, 2, 0, 3)
    row_delta = (grad_heads.astype(jnp.float32) * attn_wide).sum(-1)

    def back_step(block_index, running):
        grad_queries, grad_keys, grad_values = running
        scores, key_part, value_part = block_scores(block_index)
        probs = block_probs(scores)
        prob_low = probs.astype(jnp.bfloat16)
        grad_prob = jnp.einsum(
            "hgqd,hkd->hgqk", grad_heads, value_part, preferred_element_type=jnp.float32
        )
        grad_score = (probs * (grad_prob - row_delta[..., None]) * inv_root).astype(jnp.bfloat16)
        grad_queries = grad_queries + jnp.einsum(
            "hgqk,hkd->hgqd", grad_score, key_part, preferred_element_type=jnp.float32
        )
        key_piece = jnp.einsum(
            "hgqk,hgqd->hkd", grad_score, queries, preferred_element_type=jnp.float32
        )
        value_piece = jnp.einsum(
            "hgqk,hgqd->hkd", prob_low, grad_heads, preferred_element_type=jnp.float32
        )
        grad_keys = key_piece
        grad_values = value_piece
        return (grad_queries, grad_keys, grad_values)

    zeros_kv = jnp.zeros((KV_HEADS, length, HEAD_DIM), jnp.float32)
    grad_queries, grad_keys, grad_values = lax.fori_loop(
        0,
        needed,
        back_step,
        (jnp.zeros((KV_HEADS, group_size, rows_dev, HEAD_DIM), jnp.float32), zeros_kv, zeros_kv),
    )
    key_terms = grad_keys.transpose(1, 0, 2).reshape(1, length, KV_HEADS * HEAD_DIM)
    value_terms = grad_values.transpose(1, 0, 2).reshape(1, length, KV_HEADS * HEAD_DIM)
    key_grad, value_grad = tuple(
        (
            part.astype(jnp.float32)
            for part in in_one_piece_2(
                (key_terms.astype(jnp.bfloat16), value_terms.astype(jnp.bfloat16)),
                ("grp", "rep"),
                1,
                0,
            )
        )
    )
    query_grad = (
        grad_queries.transpose(2, 0, 1, 3)
        .reshape(1, rows_dev, HEADS * HEAD_DIM)
        .astype(jnp.bfloat16)
    )
    return (query_grad, key_grad.astype(jnp.bfloat16), value_grad.astype(jnp.bfloat16))


def solution(mesh):
    placed = (
        P("tp", ("grp", "rep"), None),
        P("tp", ("grp", "rep"), None),
        P("tp", ("grp", "rep"), None),
        P(None, ("grp", "rep"), "tp"),
        P(None, ("grp", "rep"), "tp"),
        P(None, ("grp", "rep")),
    )
    return jax.shard_map(
        shards,
        mesh=mesh,
        in_specs=placed,
        out_specs=(
            P("tp", ("grp", "rep"), None),
            P("tp", ("grp", "rep"), None),
            P("tp", ("grp", "rep"), None),
        ),
        check_vma=False,
    )
```

profile of v0, /device:TPU:4, one launch (start us, length us, event | category | flops | bytes accessed | tf_op | source)
XLA Modules:
  0.0 334.3 jit_solution(7673649836879439004)
XLA Ops:
  10.1 4.0 %copy.49 = bf16[2048,512]{0,1:T(8,128)(2,1)} copy(bf16[2048,512]{1,0:T(8,128)(2,1)} %param.17) | data formatting | bytes 4194304 | tf_op args[5]
  14.1 1.3 copy.53
  15.4 14.2 %all-to-all-start.1 = ((bf16[32,128,1]{1,2,0:T(2,128)(2,1)}), bf16[32,128,1]{1,2,0:T(2,128)(2,1)S(1)}, u32[]{:S(2)}, u32[]{:S(2)}) async-start(bf16[32,128,1]{1,2,0:T(2,128)(2,1)} %copy.53), calls=%async_computation.1 | async-start | bytes 32768 | tf_op jit(solution)/shard_map/all_to_all | solution.py:44
  29.7 2.3 copy.52
  31.9 7.8 %all-to-all-done.1 = bf16[32,128,1]{1,2,0:T(2,128)(2,1)S(1)} async-done(((bf16[32,128,1]{1,2,0:T(2,128)(2,1)}), bf16[32,128,1]{1,2,0:T(2,128)(2,1)S(1)}, u32[]{:S(2)}, u32[]{:S(2)}) %all-to-all-start.1) | async-done | bytes 8224 | tf_op jit(solution)/shard_map/all_to_all | solution.py:44
  39.7 6.7 %all-to-all-start = ((bf16[32,128,128]{1,2,0:T(8,128)(2,1)}), bf16[32,128,128]{1,2,0:T(8,128)(2,1)}, u32[]{:S(2)}, u32[]{:S(2)}) async-start(bf16[32,128,128]{1,2,0:T(8,128)(2,1)} %copy.52), calls=%async_computation | async-start | bytes 2097152 | tf_op jit(solution)/shard_map/all_to_all | solution.py:43
  47.2 1.8 copy.55
  49.0 22.4 %all-to-all-done = bf16[32,128,128]{1,2,0:T(8,128)(2,1)} async-done(((bf16[32,128,128]{1,2,0:T(8,128)(2,1)}), bf16[32,128,128]{1,2,0:T(8,128)(2,1)}, u32[]{:S(2)}, u32[]{:S(2)}) %all-to-all-start) | async-done | bytes 1048608 | tf_op jit(solution)/shard_map/all_to_all | solution.py:43
  71.5 1.5 bitcast_convert_fusion
  72.9 1.8 copy.54
  74.8 3.2 fusion.26
  78.6 1.6 copy.47
  80.2 4.2 %while.39 = (s32[]{:T(128)}, f32[4,4,128]{2,1,0:T(4,128)S(1)}, f32[4,4,128]{2,1,0:T(4,128)S(1)}, s32[]{:T(128)}, bf16[4,4,128,128]{3,2,1,0:T(8,128)(2,1)S(1)}, /...) while((s32[]{:T(128)}, f32[4,4,128]{2,1,0:T(4,128)S(1)}, ...), condition=%wide.region_3.4_spmd.clone, body=%wide.region_0.3_spmd.clone.sunk | while | flops 551687296 | bytes 18859120 | solution.py:67
  80.4 1.6 fusion.66
  82.0 2.3 exponential_reduce_fusion.2
  85.6 5.8 %while.40 = (s32[]{:T(128)}, f32[4,4,128,128]{3,2,1,0:T(8,128)}, s32[]{:T(128)}, bf16[4,4,128,128]{3,2,1,0:T(8,128)(2,1)S(1)}, bf16[4,1024,128]{2,1,0:T(8,128)(2...) while((s32[]{:T(128)}, f32[4,4,128,128]{3,2,1,0:T(8,128)}, ...), condition=%wide.region_5.6_spmd.clone, body=%wide.region_4.5_spmd.clone.sunk | while | flops 1084621952 | bytes 5006465 | solution.py:84
  85.7 5.7 %fusion.70 = f32[4,4,128,128]{3,2,1,0:T(8,128)} fusion(f32[4,4,128,128]{3,2,1,0:T(8,128)} %get-tuple-element.573, f32[4,4,128]{2,1,0:T(4,128)S(1)} %get-tuple-element.589, f32[4,4,128]{2,1,0:T(4,128)S(1)} %get-tuple-element.588, pred[128,1024]{1,0:T(8,128)(4,1)S(1)} %broadcast_compare_fusion.7, bf16[4,4,128,128]{3,2,1,0:T(8,128)(2,1)S(1)} %get-tuple-element.586, ...), kind=kOutput, calls=%fused_computation.15.clone.1 | convolution fusion | flops 1084489728 | bytes 4866048 | tf_op jit(solution)/shard_map/while/body/hgqk,hkd->hgqd/dot_general | solution.py:80
  91.4 3.0 copy.48
  95.7 141.3 %all-gather.5.cloned.1.call-done = bf16[2048,4096]{0,1:T(8,128)(2,1)} async-done(((bf16[2048,512]{0,1:T(8,128)(2,1)}), bf16[2048,4096]{0,1:T(8,128)(2,1)}) %all-gather.5.cloned.1.call-update) | async-done | bytes 16777232 | tf_op jit(solution)/shard_map/all_gather | solution.py:91
  237.0 21.9 %convert_reduce_fusion = bf16[128,2048]{1,0:T(8,128)(2,1)} fusion(bf16[2048,8,512]{0,2,1:T(8,128)(2,1)} %bitcast.142, f32[128,8,512]{2,0,1:T(8,128)} %copy.54, f32[128,8,512]{2,0,1:T(8,128)} %copy.55, bf16[128,2048,1]{0,1,2:T(8,128)(2,1)S(1)} %bitcast.145), kind=kOutput, calls=%fused_computation.36 | convolution fusion | flops 4300472320 | bytes 22020096 | tf_op jit(solution)/shard_map/tsc,dsc->std/dot_general | solution.py:101
  260.2 1.5 multiply_reduce_fusion
  265.4 11.0 %while.41 = (s32[]{:T(128)}, f32[4,4,128,128]{3,2,1,0:T(8,128)S(1)}, bf16[4,1024,128]{2,1,0:T(8,128)(2,1)}, bf16[4,1024,128]{2,1,0:T(8,128)(2,1)}, s32[]{:T(128)...) while((s32[]{:T(128)}, ...), condition=%wide.region_9.10_spmd.clone, body=%wide.region_8.9_spmd.clone.sunk | while | flops 2703623168 | bytes 51676348 | solution.py:132
  265.6 2.8 exponential_divide_fusion.2
  268.4 1.5 multiply_convert_fusion.2
  269.9 1.3 convolution_add_fusion.2
  271.2 2.6 convolution_bitcast_fusion.2
  273.8 2.6 fusion.81
  276.4 2.0 copy.64
  279.7 2.0 copy.65
  282.9 3.1 pad_maximum_fusion
  287.7 38.4 %reduce-scatter.2.cloned.1.call-done = bf16[2,128,512]{2,1,0:T(8,128)(2,1)} async-done(((bf16[2,1024,512]{2,1,0:T(8,128)(2,1)}), bf16[2,128,512]{2,1,0:T(8,128)(2,1)}) %reduce-scatter.2.cloned.1.call-update) | async-done | bytes 262160 | tf_op jit(solution)/shard_map/reduce_scatter | solution.py:24
  326.1 1.7 fusion.27
  (49 shorter events, 16.4 us)
Async XLA Ops:
  7.2 39.3 %copy-start.3 = (bf16[1,128,2048]{2,1,0:T(8,128)(2,1)S(1)}, bf16[1,128,2048]{2,1,0:T(8,128)(2,1)}, u32[]{:S(2)}) copy-start(bf16[1,128,2048]{2,1,0:T(8,128)(2,1)} %param.12) | copy-start | bytes 1572868
  7.2 67.6 %all-gather.3.cloned.1.call-start = ((), (), s32[]{:S(2)}) async-start(), calls=%async_computation.3 | async-start | bytes 2359296 | tf_op jit(solution)/shard_map/all_gather | solution.py:17
  10.1 226.9 %all-gather.5.cloned.1.call-start = ((), (), s32[]{:S(2)}) async-start(), calls=%async_computation.4 | async-start | bytes 18874368 | tf_op jit(solution)/shard_map/all_gather | solution.py:91
  15.4 24.3 %all-to-all-start.1 = ((bf16[32,128,1]{1,2,0:T(2,128)(2,1)}), bf16[32,128,1]{1,2,0:T(2,128)(2,1)S(1)}, u32[]{:S(2)}, u32[]{:S(2)}) async-start(bf16[32,128,1]{1,2,0:T(2,128)(2,1)} %copy.53), calls=%async_computation.1 | async-start | bytes 32768 | tf_op jit(solution)/shard_map/all_to_all | solution.py:44
  39.7 31.7 %all-to-all-start = ((bf16[32,128,128]{1,2,0:T(8,128)(2,1)}), bf16[32,128,128]{1,2,0:T(8,128)(2,1)}, u32[]{:S(2)}, u32[]{:S(2)}) async-start(bf16[32,128,128]{1,2,0:T(8,128)(2,1)} %copy.52), calls=%async_computation | async-start | bytes 2097152 | tf_op jit(solution)/shard_map/all_to_all | solution.py:43
  46.4 279.7 %reduce-scatter.2.cloned.1.call-start = ((), (), s32[]{:S(2)}) async-start(), calls=%async_computation.5 | async-start | bytes 2359296 | tf_op jit(solution)/shard_map/reduce_scatter | solution.py:24
  91.4 167.5 %copy-start = (bf16[4,1024,128]{2,1,0:T(8,128)(2,1)}, bf16[4,1024,128]{2,1,0:T(8,128)(2,1)S(1)}, u32[]{:S(2)}) copy-start(bf16[4,1024,128]{2,1,0:T(8,128)(2,1)S(1)} %get-tuple-element.647) | copy-start | bytes 3145732
  260.2 1.6 copy-start.2
  265.6 2.8 copy-start.1
Sparse Core Ops, SparseCore 0:
  10.3 46.4 all-gather.2
  58.5 178.4 all-gather.4
  286.2 39.9 reduce-scatter.1
where the time goes:
time: 335 us; the launch traced here: 334 us
  waiting for transfers between devices  210 us (63%)
  matrix products  39.9 us (12%)
  local copies, waits for them, and re-layouts  38.4 us (11%)
  starting transfers between devices  21 us (6%)
  between operations  13.9 us (4%)
  other arithmetic  11 us (3%)
    all_gather x1, waiting for transfers between devices, shards(): shard_piece = lax.all_gather(projection, ('grp', 'rep'), axis=1, tiled=True)  141 us
    reduce_scatter x1, waiting for transfers between devices, in_one_piece_2(): whole = lax.psum_scatter(both, axis, scatter_dimension=dim, tiled=True)  38.4 us
    all_to_all x1, waiting for transfers between devices, shards(): lax.all_to_all(teacher_codes, 'tp', split_axis=0, concat_axis=2, tiled=True)  22.4 us
    dot_general x1, matrix products, shards(): jnp.einsum('tsc,dsc->std', errors, shaped, preferred_element_type=jnp.flo...  21.9 us
    all_to_all x1, starting transfers between devices, shards(): lax.all_to_all(teacher_scales, 'tp', split_axis=0, concat_axis=2, tiled=T...  14.2 us
    unnamed x16, local copies, waits for them, and re-layouts  13.8 us
    all_to_all x1, waiting for transfers between devices, shards(): lax.all_to_all(teacher_scales, 'tp', split_axis=0, concat_axis=2, tiled=T...  7.78 us
  transfers between devices with their start and end apart: 5, of which 4 were waited for; matrix products, arithmetic and copies ran while one was open for 11% of the time, Pallas kernels for 0%

commit v1 on v0

--- a/solution.py
+++ b/solution.py
@@ -3,12 +3,20 @@
 import jax.numpy as jnp
 from jax import lax
 from jax.sharding import PartitionSpec as P
+from jax.lax import all_to_all, axis_size
 
 HEADS = 16
 KV_HEADS = 4
 HEAD_DIM = 128
 QBLOCK = 128
 masked_low = -1e30
+
+
+def report_the_skins(s0):
+    table = []
+    for _ in range(axis_size(("grp", "rep"))):
+        table.append(s0)
+    return jnp.concatenate(all_to_all(jnp.stack(table), ("grp", "rep"), 0, 0), axis=1)
 
 
 def in_one_piece(arrays, axis, dim, along):
@@ -88,7 +96,7 @@
         attn_wide.transpose(2, 0, 1, 3).reshape(rows_dev, HEADS * HEAD_DIM).astype(jnp.bfloat16)
     )
     col_width = projection.shape[1]
-    shard_piece = lax.all_gather(projection, ("grp", "rep"), axis=1, tiled=True)
+    shard_piece = report_the_skins(projection)
     pieces = shard_piece.shape[1] // col_width
     shaped = shard_piece.reshape(shard_piece.shape[0], pieces, col_width)
     approx = jnp.einsum("td,dsc->tsc", attn_low, shaped, preferred_element_type=jnp.float32)

time: 335 us -> 558 us (1.67)
  waiting for transfers between devices: 210 us -> 400 us
  blocking collectives: 0 us -> 26.2 us
    all_to_all x1, waiting for transfers between devices: 22.4 us -> 256 us  [report_the_skins(): all_to_all(jnp.stack(table), ('grp', 'rep'), 0, 0)]
    all_gather x1 -> x0, waiting for transfers between devices: 141 us -> none  [shards(): shard_piece = lax.all_gather(projection, ('grp', 'rep'), axis=1, tiled=True)]
    all_gather x1, waiting for transfers between devices: 0.01 us -> 99.8 us  [in_one_piece(): whole = lax.all_gather(both, axis, axis=dim, tiled=True)]
    all_to_all x0 -> x1, blocking collectives: none -> 26.2 us  [shards(): lax.all_to_all(teacher_codes, 'tp', split_axis=0, concat_axis=2, tiled=True)]
    another operation x2 -> x3, local copies, waits for them, and re-layouts: 1.27 us -> 8.02 us  [the longest x1 6.82 us: report_the_skins(): jnp.stack(table)]
    unnamed x16 -> x19, local copies, waits for them, and re-layouts: 13.8 us -> 7.33 us
  transfers between devices with their start and end apart: 5 -> 4, of which waited for: 4 -> 4; matrix products, arithmetic and copies ran while one was open for 11% -> 5% of each run, Pallas kernels for 0% -> 0%
where the time goes in v1:
time: 558 us
  waiting for transfers between devices  400 us (72%)
  matrix products  42 us (8%)
  local copies, waits for them, and re-layouts  38.2 us (7%)
  blocking collectives  26.2 us (5%)
  starting transfers between devices  26 us (5%)
  between operations  14.3 us (3%)
  other arithmetic  11 us (2%)
    all_to_all x1, waiting for transfers between devices, report_the_skins(): all_to_all(jnp.stack(table), ('grp', 'rep'), 0, 0)  256 us
    all_gather x1, waiting for transfers between devices, in_one_piece(): whole = lax.all_gather(both, axis, axis=dim, tiled=True)  99.8 us
    reduce_scatter x1, waiting for transfers between devices, in_one_piece_2(): whole = lax.psum_scatter(both, axis, scatter_dimension=dim, tiled=True)  35.1 us
    all_to_all x1, blocking collectives, shards(): lax.all_to_all(teacher_codes, 'tp', split_axis=0, concat_axis=2, tiled=True)  26.2 us
    dot_general x1, matrix products, shards(): jnp.einsum('tsc,dsc->std', errors, shaped, preferred_element_type=jnp.flo...  24.1 us
    all_to_all x1, starting transfers between devices, shards(): lax.all_to_all(teacher_scales, 'tp', split_axis=0, concat_axis=2, tiled=T...  14.2 us
    all_to_all x1, starting transfers between devices, report_the_skins(): all_to_all(jnp.stack(table), ('grp', 'rep'), 0, 0)  11.7 us
  transfers between devices with their start and end apart: 4, of which 4 were waited for; matrix products, arithmetic and copies ran while one was open for 5% of the time, Pallas kernels for 0%

profile of v1, /device:TPU:4, one launch (start us, length us, event | category | flops | bytes accessed | tf_op | source)
XLA Modules:
  0.0 557.6 jit_solution(12981331852601185672)
XLA Ops:
  8.5 14.2 %all-to-all-start.2 = ((bf16[32,128,1]{1,2,0:T(2,128)(2,1)}), bf16[32,128,1]{1,2,0:T(2,128)(2,1)S(1)}, u32[]{:S(2)}, u32[]{:S(2)}) async-start(bf16[32,128,1]{1,2,0:T(2,128)(2,1)} %copy.49), calls=%async_computation.2 | async-start | bytes 32768 | tf_op jit(solution)/shard_map/all_to_all | solution.py:52
  22.7 1.6 copy.48
  24.3 8.4 %all-to-all-done.2 = bf16[32,128,1]{1,2,0:T(2,128)(2,1)S(1)} async-done(((bf16[32,128,1]{1,2,0:T(2,128)(2,1)}), bf16[32,128,1]{1,2,0:T(2,128)(2,1)S(1)}, u32[]{:S(2)}, u32[]{:S(2)}) %all-to-all-start.2) | async-done | bytes 8224 | tf_op jit(solution)/shard_map/all_to_all | solution.py:52
  32.7 26.2 %all_to_all.23 = bf16[32,128,128]{1,2,0:T(8,128)(2,1)} all-to-all(bf16[32,128,128]{1,2,0:T(8,128)(2,1)S(1)} %copy.48), channel_id=1, replica_groups=mesh['grp'=4,'tp'=32,'rep'=2] {'tp'}, dimensions={0} | all-to-all | bytes 2097152 | tf_op jit(solution)/shard_map/all_to_all | solution.py:51
  59.0 6.8 %stack.2 = bf16[8,2048,512]{2,1,0:T(8,128)(2,1)} broadcast(bf16[2048,512]{1,0:T(8,128)(2,1)} %param.17), dimensions={1,2} | broadcast | bytes 18874368 | tf_op jit(solution)/shard_map/stack | solution.py:19
  65.8 11.7 %all-to-all-start = ((bf16[8,2048,512]{2,1,0:T(8,128)(2,1)}), bf16[8,2048,512]{2,1,0:T(8,128)(2,1)}, u32[]{:S(2)}, u32[]{:S(2)}) async-start(bf16[8,2048,512]{2,1,0:T(8,128)(2,1)} %stack.2), calls=%async_computation | async-start | bytes 33554432 | tf_op jit(solution)/shard_map/all_to_all | solution.py:19
  79.3 1.9 copy.51
  81.2 1.5 bitcast_convert_fusion
  82.7 1.9 copy.50
  84.5 99.8 %all-gather.2.cloned.1.call-done = bf16[2,1024,512]{1,2,0:T(8,128)(2,1)} async-done(((bf16[2,128,512]{1,2,0:T(8,128)(2,1)}), bf16[2,1024,512]{1,2,0:T(8,128)(2,1)}) %all-gather.2.cloned.1.call-update) | async-done | bytes 2097168 | tf_op jit(solution)/shard_map/all_gather | solution.py:25
  184.3 2.7 fusion.36
  187.7 1.6 copy.45
  189.4 4.2 while.39
  189.5 1.6 fusion.65
  191.1 2.3 exponential_reduce_fusion.2
  194.6 5.7 %while.40 = (s32[]{:T(128)}, f32[4,4,128,128]{3,2,1,0:T(8,128)}, s32[]{:T(128)}, bf16[4,4,128,128]{3,2,1,0:T(8,128)(2,1)S(1)}, bf16[4,1024,128]{2,1,0:T(8,128)(2...) while((s32[]{:T(128)}, f32[4,4,128,128]{3,2,1,0:T(8,128)}, ...), condition=%wide.region_5.6_spmd.clone, body=%wide.region_4.5_spmd.clone.sunk | while | flops 1084621952 | bytes 5006465 | solution.py:92
  194.8 5.6 fusion.69
  200.4 2.9 copy.46
  204.6 256.5 %all-to-all-done = bf16[8,2048,512]{2,1,0:T(8,128)(2,1)} async-done(((bf16[8,2048,512]{2,1,0:T(8,128)(2,1)}), bf16[8,2048,512]{2,1,0:T(8,128)(2,1)}, u32[]{:S(2)}, u32[]{:S(2)}) %all-to-all-start) | async-done | bytes 16777248 | tf_op jit(solution)/shard_map/all_to_all | solution.py:19
  461.0 24.1 %convert_reduce_fusion = bf16[128,2048]{1,0:T(8,128)(2,1)} fusion(bf16[8,2048,512]{2,1,0:T(8,128)(2,1)} %all-to-all-done, f32[128,8,512]{2,0,1:T(8,128)} %copy.50, f32[128,8,512]{2,0,1:T(8,128)} %copy.51, bf16[128,2048,1]{0,1,2:T(8,128)(2,1)S(1)} %bitcast.143), kind=kOutput, calls=%fused_computation.40 | convolution fusion | flops 4300472320 | bytes 22020096 | tf_op jit(solution)/shard_map/tsc,dsc->std/dot_general | solution.py:109
  486.4 1.5 multiply_reduce_fusion
  491.7 11.0 %while.41 = (s32[]{:T(128)}, f32[4,4,128,128]{3,2,1,0:T(8,128)S(1)}, bf16[4,1024,128]{2,1,0:T(8,128)(2,1)}, bf16[4,1024,128]{2,1,0:T(8,128)(2,1)}, s32[]{:T(128)...) while((s32[]{:T(128)}, ...), condition=%wide.region_9.10_spmd.clone, body=%wide.region_8.9_spmd.clone.sunk | while | flops 2703623168 | bytes 51676348 | solution.py:140
  491.8 2.8 exponential_divide_fusion.2
  494.6 1.5 multiply_convert_fusion.2
  496.1 1.3 convolution_add_fusion.2
  497.4 2.6 convolution_bitcast_fusion.2
  500.0 2.6 fusion.80
  502.7 2.0 copy.59
  505.9 2.0 copy.60
  509.2 3.1 pad_maximum_fusion
  514.0 35.1 %reduce-scatter.2.cloned.1.call-done = bf16[2,128,512]{2,1,0:T(8,128)(2,1)} async-done(((bf16[2,1024,512]{2,1,0:T(8,128)(2,1)}), bf16[2,128,512]{2,1,0:T(8,128)(2,1)}) %reduce-scatter.2.cloned.1.call-update) | async-done | bytes 262160 | tf_op jit(solution)/shard_map/reduce_scatter | solution.py:32
  549.1 1.7 fusion.37
  (51 shorter events, 15.8 us)
Async XLA Ops:
  8.5 24.3 %all-to-all-start.2 = ((bf16[32,128,1]{1,2,0:T(2,128)(2,1)}), bf16[32,128,1]{1,2,0:T(2,128)(2,1)S(1)}, u32[]{:S(2)}, u32[]{:S(2)}) async-start(bf16[32,128,1]{1,2,0:T(2,128)(2,1)} %copy.49), calls=%async_computation.2 | async-start | bytes 32768 | tf_op jit(solution)/shard_map/all_to_all | solution.py:52
  65.8 11.7 %copy-start.4 = (bf16[1,128,512]{2,1,0:T(8,128)(2,1)S(1)}, bf16[1,128,512]{2,1,0:T(8,128)(2,1)}, u32[]{:S(2)}) copy-start(bf16[1,128,512]{2,1,0:T(8,128)(2,1)} %param.13) | copy-start | bytes 393220
  65.8 11.9 %copy-start.5 = (bf16[1,128,512]{2,1,0:T(8,128)(2,1)S(1)}, bf16[1,128,512]{2,1,0:T(8,128)(2,1)}, u32[]{:S(2)}) copy-start(bf16[1,128,512]{2,1,0:T(8,128)(2,1)} %param.14) | copy-start | bytes 393220
  65.8 12.8 %copy-start.3 = (bf16[1,128,2048]{2,1,0:T(8,128)(2,1)S(1)}, bf16[1,128,2048]{2,1,0:T(8,128)(2,1)}, u32[]{:S(2)}) copy-start(bf16[1,128,2048]{2,1,0:T(8,128)(2,1)} %param.12) | copy-start | bytes 1572868
  65.8 395.2 %all-to-all-start = ((bf16[8,2048,512]{2,1,0:T(8,128)(2,1)}), bf16[8,2048,512]{2,1,0:T(8,128)(2,1)}, u32[]{:S(2)}, u32[]{:S(2)}) async-start(bf16[8,2048,512]{2,1,0:T(8,128)(2,1)} %stack.2), calls=%async_computation | async-start | bytes 33554432 | tf_op jit(solution)/shard_map/all_to_all | solution.py:19
  77.5 106.9 %all-gather.2.cloned.1.call-start = ((), (), s32[]{:S(2)}) async-start(), calls=%async_computation.4 | async-start | bytes 2359296 | tf_op jit(solution)/shard_map/all_gather | solution.py:25
  78.5 470.5 %reduce-scatter.2.cloned.1.call-start = ((), (), s32[]{:S(2)}) async-start(), calls=%async_computation.5 | async-start | bytes 2359296 | tf_op jit(solution)/shard_map/reduce_scatter | solution.py:32
  200.3 284.7 %copy-start = (bf16[4,1024,128]{2,1,0:T(8,128)(2,1)}, bf16[4,1024,128]{2,1,0:T(8,128)(2,1)S(1)}, u32[]{:S(2)}) copy-start(bf16[4,1024,128]{2,1,0:T(8,128)(2,1)S(1)} %get-tuple-element.647) | copy-start | bytes 3145732
  486.4 1.6 copy-start.2
  491.8 2.8 copy-start.1
Sparse Core Ops, SparseCore 0:
  80.6 103.7 all-gather.1
  512.4 36.6 reduce-scatter.1
